TPU v7x, 32 devices: a whole 2x2x4 slice. The times are simulated.
32 devices in a mesh: gx: 4 (over y, x), gy: 8 (over z, core).
Axes of the slice: x: 2, y: 2, z: 4, core: 2. Of those that a mesh axis runs over, the one named last changes fastest.
Arguments:
- primal: float32 [4, 27, 16384], P(None, None, ('gx', 'gy')), may hold values from -6 to 6
- adjoint: float32 [4, 27, 16384], P(None, None, ('gx', 'gy')), may hold values from -6 to 6
- source: float32 [4, 27, 16384], P(None, None, ('gx', 'gy')), may hold values from -6 to 6
- coefficient: float32 [16384], P(('gx', 'gy')), may hold values from 0.3 to 3
- levels: int32 [16384], P(('gx', 'gy')), may hold values from 0 to 3
- recon: float32 [7, 125, 27], replicated, may hold values from -0.4375 to 0.4375
- stiffness: float32 [125, 27], replicated, may hold values from -1.25 to 1.25
- interp: float32 [125, 27], replicated, may hold values from -1.25 to 1.25
- flux: float32 [6, 25, 27], replicated, may hold values from -1.25 to 1.25
- face_eval: float32 [6, 25, 125], replicated, may hold values from -0.5 to 0.5
- child_interp: float32 [4, 25, 25], replicated, may hold values from -1.25 to 1.25
- ghost_send: int32 [32, 8, 32], P(('gx', 'gy')), may hold values from -1 to 511, as said below
- edge_send: int32 [32, 2, 16], P(('gx', 'gy')), may hold values from -1 to 511, as said below
- neighbor_slot: int32 [6, 16384], P(None, ('gx', 'gy')), may hold values from -1 to 799, as said below
- neighbor_child: int32 [6, 16384], P(None, ('gx', 'gy')), may hold values from 0 to 4, as said below
- hang_send: int32 [2, 32, 8, 8], P(None, ('gx', 'gy')), may hold values from -1 to 511, as said below
- hang_recv: int32 [3, 32, 8, 8], P(None, ('gx', 'gy')), may hold values from -1 to 511, as said below
Outputs:
- cell_indicator: float32 [4, 16384], P(None, ('gx', 'gy'))
- face_indicator: float32 [4, 16384], P(None, ('gx', 'gy'))
Inputs may be any that keep to these rules, and one draw needn't show every extreme that they name: `ghost_send`: the gy index of a device numbers a block of a cube of blocks with side S, the cube root of 8: index = G(c0) + S * G(c1) + S * S * G(c2) for block coordinates c0, c1, c2, where G(p) = p xor (p // 2) is the Gray code, so face-adjacent blocks differ in one bit of the index. Row [r, p] lists the local cells that device r sends to the device with its gx index and gy index p, live ids first, then -1. Only the up to six blocks face-adjacent to r's block get live ids, between 16 and 32 of them, and exactly 32 go to the neighbour one step up along coordinate 0 wherever it exists. `edge_send`: row [r, 0] lists the local cells sent to the device one gx index lower with the same gy index, row [r, 1] those sent to the one higher, live ids first, then -1; where that device exists there are 8 to 16 live ids, and exactly 16 towards the lower one; otherwise the row is all -1. `neighbor_slot`: every slot that is not -1 points at a live entry: a cell of the device itself, a live entry of a gy peer's ghost_send row for this device, or a live entry of a gx neighbour's edge_send row towards this device. `neighbor_child`: 4 means a neighbour of the same level. `hang_send`: [0, r, p, t] is a local cell of device r and [1, r, p, t] one of its faces, both -1 after the live slots; live slots go only to face-adjacent gy peers (as for ghost_send), at most 8 to one peer, and the device with gy index 0 sends exactly 8 to each of its face-adjacent peers. `hang_recv`: [:, q, p, t] describes what device q receives in slot t from the device with its gx index and gy index p: a local coarse cell, its face (the opposite of the sender's fine face) and a child position 0 to 3; all three are -1 exactly where the sender's slot is empty.
All inputs are finite; a program needn't handle non-finite values.
Results may differ from a plain program's by a relative error of at most 0.0003.
Values sent between devices are 32-bit elements; how exact they have to be, the bound alone decides.
No kernel may reach another device: no remote copies, remote signals or barrier semaphores. Data moves between devices by JAX's collectives and lax.ppermute only.
A program may use at most 128 MiB of HBM per device.

v0:
```python
import math

import jax
import jax.numpy as jnp
from jax import lax
from jax.experimental import pallas as pl
from jax.experimental.pallas import tpu as pltpu
from jax.sharding import PartitionSpec as P

F32 = jnp.float32
BF16 = jnp.bfloat16
FACES = 6
CHILDREN = 4
KINDS = CHILDREN + 1


def up(value, unit):
    return -(-value // unit) * unit


def dot(a, b):
    return lax.dot_general(a, b, (((1,), (0,)), ((), ())), preferred_element_type=F32)


def dot_nt(a, b):
    return lax.dot_general(a, b, (((1,), (1,)), ((), ())), preferred_element_type=F32)


def split(x):
    hi = x.astype(BF16)
    return hi, (x - hi.astype(F32)).astype(BF16)


def iota(shape, axis):
    return lax.broadcasted_iota(jnp.int32, shape, axis)


def column(row):
    n = row.shape[1]
    spread = jnp.broadcast_to(row.astype(F32), (n, n))
    eye = iota((n, n), 0) == iota((n, n), 1)
    return jnp.sum(jnp.where(eye, spread, 0.0), axis=1, keepdims=True).astype(jnp.int32)


def onehot(mask):
    return jnp.where(mask, 1.0, 0.0).astype(BF16)


def placed_at(rows, width, offsets):
    rel = iota((rows, width), 1) - iota((rows, width), 0)
    hit = rel == offsets[0]
    for offset in offsets[1:]:
        hit = hit | (rel == offset)
    return onehot(hit)


class Sizes:
    def __init__(self, primal, ghost_send, edge_send, hang_send, recon, flux, peers):
        self.k, self.d, self.c = primal.shape
        self.dp = up(self.d, 32)
        self.rows = self.k * self.dp
        self.gs = ghost_send.shape[2]
        self.xs = edge_send.shape[2]
        self.hs = hang_send.shape[3]
        self.peers = peers
        self.bits = peers.bit_length() - 1
        self.msg = self.gs + self.hs
        self.remote = up(self.bits * self.gs + 2 * self.xs, 128)
        self.hp = 32
        while self.hp < self.bits * self.hs:
            self.hp *= 2
        self.hl = up(self.k * self.hp, 128)
        self.q = recon.shape[1]
        self.qp = up(self.q, 128)
        self.p = flux.shape[1]
        self.pp = up(self.p, 32)


def pack_kernel(n, primal, adjoint, ghost, edge, hang, *refs):
    outs, (data, picks) = refs[: n.bits + 2], refs[n.bits + 2 :]
    own = lax.axis_index("gy")
    data[...] = jnp.zeros(data.shape, F32)
    for k in range(n.k):
        data[k * n.dp : k * n.dp + n.d, :] = primal[k]
        data[n.rows + k * n.dp : n.rows + k * n.dp + n.d, :] = adjoint[k]
    for b in range(n.bits):
        partner = own ^ (1 << b)
        g = column(ghost[0, pl.ds(partner, 1), :])
        h = column(hang[0, 0, pl.ds(partner, 1), :])
        picks[b * n.msg : b * n.msg + n.gs, :] = jnp.where(g == iota((n.gs, n.c), 1), 1.0, 0.0)
        picks[b * n.msg + n.gs : (b + 1) * n.msg, :] = jnp.where(h == iota((n.hs, n.c), 1), 1.0, 0.0)
    base = n.bits * n.msg
    for side in range(2):
        e = column(edge[0, side : side + 1, :])
        picks[base + side * n.xs : base + (side + 1) * n.xs, :] = jnp.where(e == iota((n.xs, n.c), 1), 1.0, 0.0)
    hi, lo = split(data[...])
    sel = picks[...].astype(BF16)
    got = dot_nt(sel, hi) + dot_nt(sel, lo)
    for b in range(n.bits):
        outs[b][...] = got[b * n.msg : (b + 1) * n.msg]
    for side in range(2):
        outs[n.bits + side][...] = got[base + side * n.xs : base + (side + 1) * n.xs]


def local_kernel(
    n, primal, adjoint, source, coefficient, slots, hang_recv, recon, stiffness, interp, flux, face_eval, child,
    gathered, own2, residual, rw, mw, hw, fe, hcol, hrow, data, stack, faces, weights,
):
    own = lax.axis_index("gy")
    data[...] = jnp.zeros(data.shape, F32)
    for k in range(n.k):
        data[k * n.dp : k * n.dp + n.d, :] = primal[k]
        data[n.rows + k * n.dp : n.rows + k * n.dp + n.d, :] = adjoint[k]
    hi, lo = split(data[...])
    both = jnp.concatenate([hi, lo], axis=0)
    own2[...] = both
    for f in range(FACES):
        pick = onehot(slots[f : f + 1, :] == iota((n.c, n.c), 0))
        gathered[f] = dot(both, pick).astype(BF16)
    i_hi, i_lo = split(interp[...])
    s_hi, s_lo = split(stiffness[...])
    coeff = coefficient[...]
    for k in range(n.k):
        src_hi, src_lo = split(source[k])
        u_hi, u_lo = split(primal[k] * coeff)
        res = dot(i_hi, src_hi) + dot(i_hi, src_lo) + dot(i_lo, src_hi)
        res = res - (dot(s_hi, u_hi) + dot(s_hi, u_lo) + dot(s_lo, u_hi))
        residual[k, : n.q, :] = res
        if n.qp > n.q:
            residual[k, n.q :, :] = jnp.zeros((n.qp - n.q, n.c), F32)
    width = rw.shape[1]
    acc_hi = jnp.zeros((n.q, width), F32)
    acc_lo = jnp.zeros((n.q, width), F32)
    for m in range(1 + FACES):
        w_hi, w_lo = split(recon[m])
        acc_hi += dot(w_hi, placed_at(n.d, width, (2 * m * n.dp, (2 * m + 1) * n.dp)))
        acc_lo += dot(w_lo, placed_at(n.d, width, (2 * m * n.dp,)))
    weights[...] = jnp.zeros(weights.shape, F32)
    weights[: n.q, :] = acc_hi
    weights[n.qp : n.qp + n.q, :] = acc_lo
    rw[...] = weights[...].astype(BF16)
    stack[...] = jnp.zeros(stack.shape, F32)
    for h in range(CHILDREN):
        stack[0, h * n.pp : h * n.pp + n.p, : n.p] = child[h]
        stack[3, h * n.pp : h * n.pp + n.p, : n.p] = child[h].T
    width = mw.shape[2]
    for f in range(FACES):
        child_rows = stack[0, : CHILDREN * n.pp, : n.p]
        stack[1, : CHILDREN * n.pp, : n.d] = lax.dot_general(
            child_rows, flux[f ^ 1], (((1,), (0,)), ((), ())),
            precision=lax.Precision.HIGHEST, preferred_element_type=F32,
        )
        stack[1, CHILDREN * n.pp : CHILDREN * n.pp + n.p, : n.d] = flux[f ^ 1]
        for h in range(KINDS):
            stack[2, h * n.pp : h * n.pp + n.p, : n.d] = flux[f]
        m_hi, m_lo = split(stack[1, :, : n.d])
        f_hi, f_lo = split(stack[2, :, : n.d])
        mw[f] = (
            dot(m_hi, placed_at(n.d, width, (0, n.dp)))
            + dot(m_lo, placed_at(n.d, width, (2 * n.dp,)))
            + dot(f_hi, placed_at(n.d, width, (3 * n.dp, 4 * n.dp)))
            + dot(f_lo, placed_at(n.d, width, (5 * n.dp,)))
        ).astype(BF16)
        turned = lax.dot_general(
            stack[3, : CHILDREN * n.pp, : n.p], flux[f ^ 1], (((1,), (0,)), ((), ())),
            precision=lax.Precision.HIGHEST, preferred_element_type=F32,
        )
        t_hi, t_lo = split(turned)
        hw[f] = (
            dot(t_hi, placed_at(n.d, 3 * n.dp, (0, n.dp))) + dot(t_lo, placed_at(n.d, 3 * n.dp, (2 * n.dp,)))
        ).astype(BF16)
    faces[...] = jnp.zeros(faces.shape, F32)
    for f in range(FACES):
        faces[f * n.pp : f * n.pp + n.p, : n.q] = face_eval[f]
    e_hi, e_lo = split(faces[...])
    rows = FACES * n.pp
    fe[:rows, : n.qp] = e_hi
    fe[:rows, n.qp :] = e_hi
    fe[rows:, : n.qp] = e_lo
    fe[rows:, n.qp :] = jnp.zeros((rows, n.qp), BF16)
    hcol[...] = jnp.full(hcol.shape, -1.0, F32)
    for which in range(3):
        for b in range(n.bits):
            partner = own ^ (1 << b)
            col = column(hang_recv[which, 0, pl.ds(partner, 1), :]).astype(F32)
            for k in range(n.k):
                at = k * n.hp + b * n.hs
                hcol[at : at + n.hs, which * 128 : (which + 1) * 128] = jnp.broadcast_to(col, (n.hs, 128))
    eye = iota((n.hl, n.hl), 0) == iota((n.hl, n.hl), 1)
    for which in range(3):
        spread = jnp.broadcast_to(hcol[:, which * 128 : which * 128 + 1], (n.hl, n.hl))
        hrow[which : which + 1, :] = jnp.sum(jnp.where(eye, spread, 0.0), axis=0, keepdims=True)


def final_kernel(n, gathered, own2, residual, rw, mw, hw, fe, hcol, hrow, slots, kinds, levels, *refs):
    msgs = refs[: n.bits + 2]
    cell_out, face_out, incoming, hanging, zbuf, totals = refs[n.bits + 2 :]
    own = lax.axis_index("gy")
    incoming[...] = jnp.zeros(incoming.shape, F32)
    hanging[...] = jnp.zeros(hanging.shape, F32)
    for b in range(n.bits):
        incoming[b * n.gs : (b + 1) * n.gs, :] = msgs[b][: n.gs, :]
        hanging[b * n.hs : (b + 1) * n.hs, :] = msgs[b][n.gs :, : n.rows]
    base = n.bits * n.gs
    for side in range(2):
        incoming[base + side * n.xs : base + (side + 1) * n.xs, :] = msgs[n.bits + side][...]
    r_hi, r_lo = split(incoming[...].T)
    remote = jnp.concatenate([r_hi, r_lo], axis=0)
    place = iota((n.remote, n.c), 0)
    code = n.c + n.peers * n.gs + place - base
    for b in range(n.bits):
        inside = (place >= b * n.gs) & (place < (b + 1) * n.gs)
        code = jnp.where(inside, n.c + (own ^ (1 << b)) * n.gs + place - b * n.gs, code)
    code = jnp.where(place < base + 2 * n.xs, code, -2)
    hang_t = hanging[...].T
    if n.hl > hang_t.shape[1]:
        hang_t = jnp.concatenate([hang_t, jnp.zeros((n.rows, n.hl - hang_t.shape[1]), F32)], axis=1)
    spread = hang_t[: n.dp]
    for k in range(1, n.k):
        spread = spread + pltpu.roll(hang_t[k * n.dp : (k + 1) * n.dp], k * n.hp, 1)
    h_hi, h_lo = split(spread)
    h_in = jnp.concatenate([h_hi, h_lo, h_hi], axis=0)
    lifted = jnp.zeros((n.pp, n.hl), F32)
    for f in range(FACES):
        term = dot(hw[f], h_in)
        for h in range(CHILDREN):
            hit = (hrow[1:2, :] == f) & (hrow[2:3, :] == h)
            lifted = lifted + jnp.where(hit, term[h * n.pp : (h + 1) * n.pp], 0.0)
    lane = iota((n.pp, n.hl), 1)
    blocks = [
        jnp.where((lane >= k * n.hp) & (lane < (k + 1) * n.hp), lifted, 0.0) for k in range(n.k)
    ]
    l_hi, l_lo = split(jnp.concatenate(blocks, axis=0))
    target = (hcol[:, :1] + hcol[:, 128:129] * n.c).astype(jnp.int32)
    half = 2 * n.rows
    for k in range(n.k):
        for part in range(2):
            at = part * half + n.rows + k * n.dp
            zbuf[k, part * n.dp : (part + 1) * n.dp, :] = own2[at : at + n.dp, :]
    for f in range(FACES):
        got = gathered[f].astype(F32) + dot(remote, onehot(slots[f : f + 1, :] == code))
        got = got.astype(BF16)
        back = onehot(target - f * n.c == iota((n.hl, n.c), 1))
        extra = dot(l_hi, back) + dot(l_lo, back)
        kind = kinds[f : f + 1, :]
        for k in range(n.k):
            z_at = n.rows + k * n.dp
            for part in range(2):
                at = (2 * (1 + f) + part) * n.dp
                zbuf[k, at : at + n.dp, :] = got[part * half + z_at : part * half + z_at + n.dp]
            u_at = k * n.dp
            near_hi = got[u_at : u_at + n.dp]
            near_lo = got[half + u_at : half + u_at + n.dp]
            own_hi = own2[u_at : u_at + n.dp, :]
            own_lo = own2[half + u_at : half + u_at + n.dp, :]
            stacked = jnp.concatenate([near_hi, near_lo, near_hi, own_hi, own_lo, own_hi], axis=0)
            term = dot(mw[f], stacked)
            total = extra[k * n.pp : (k + 1) * n.pp]
            chosen = term[CHILDREN * n.pp :]
            for h in range(CHILDREN):
                chosen = jnp.where(kind == h, term[h * n.pp : (h + 1) * n.pp], chosen)
            totals[k, f * n.pp : (f + 1) * n.pp, :] = total + chosen
    size = jnp.exp2(-levels[...].astype(F32))
    rows = FACES * n.pp
    for k in range(n.k):
        both = dot(rw[...], zbuf[k])
        weight = both[: n.qp] + both[n.qp :]
        part = jnp.sum(residual[k] * weight, axis=0, keepdims=True)
        cell_out[k : k + 1, :] = size * part / math.sqrt(n.q)
        w_hi, w_lo = split(weight)
        both = dot(fe[...], jnp.concatenate([w_hi, w_lo], axis=0))
        face_weight = both[:rows] + both[rows:]
        part = jnp.sum(totals[k] * face_weight, axis=0, keepdims=True)
        face_out[k : k + 1, :] = size * part / math.sqrt(FACES * n.p)


def params():
    return pltpu.CompilerParams(vmem_limit_bytes=56 * 2**20)


def shards(
    primal, adjoint, source, coefficient, levels, recon, stiffness, interp, flux, face_eval, child_interp,
    ghost_send, edge_send, neighbor_slot, neighbor_child, hang_send, hang_recv,
):
    n = Sizes(primal, ghost_send, edge_send, hang_send, recon, flux, lax.axis_size("gy"))
    shape = jax.ShapeDtypeStruct
    lanes = 2 * n.rows
    sent = pl.pallas_call(
        lambda *refs: pack_kernel(n, *refs),
        out_shape=[shape((n.msg, lanes), F32)] * n.bits + [shape((n.xs, lanes), F32)] * 2,
        scratch_shapes=[
            pltpu.VMEM((lanes, n.c), F32),
            pltpu.VMEM((n.bits * n.msg + 2 * n.xs, n.c), F32),
        ],
        compiler_params=params(),
        name="pack",
    )(primal, adjoint, ghost_send, edge_send, hang_send)
    msgs = []
    for b in range(n.bits):
        pairs = [(i, i ^ (1 << b)) for i in range(n.peers)]
        msgs.append(lax.ppermute(sent[b], "gy", pairs))
    steps = lax.axis_size("gx")
    rising = [(i, i + 1) for i in range(steps - 1)]
    msgs.append(lax.ppermute(sent[n.bits + 1], "gx", rising))
    msgs.append(lax.ppermute(sent[n.bits], "gx", [(j, i) for i, j in rising]))
    local = pl.pallas_call(
        lambda *refs: local_kernel(n, *refs),
        out_shape=[
            shape((FACES, 2 * lanes, n.c), BF16),
            shape((2 * lanes, n.c), BF16),
            shape((n.k, n.qp, n.c), F32),
            shape((2 * n.qp, 2 * (1 + FACES) * n.dp), BF16),
            shape((FACES, KINDS * n.pp, 6 * n.dp), BF16),
            shape((FACES, CHILDREN * n.pp, 3 * n.dp), BF16),
            shape((2 * FACES * n.pp, 2 * n.qp), BF16),
            shape((n.hl, 3 * 128), F32),
            shape((8, n.hl), F32),
        ],
        scratch_shapes=[
            pltpu.VMEM((lanes, n.c), F32),
            pltpu.VMEM((4, KINDS * n.pp, 128), F32),
            pltpu.VMEM((FACES * n.pp, n.qp), F32),
            pltpu.VMEM((2 * n.qp, 2 * (1 + FACES) * n.dp), F32),
        ],
        compiler_params=params(),
        cost_estimate=pl.CostEstimate(flops=10**10, bytes_accessed=10**7, transcendentals=0),
        name="local",
    )(
        primal, adjoint, source, coefficient.reshape(1, n.c), neighbor_slot, hang_recv,
        recon, stiffness, interp, flux, face_eval, child_interp,
    )
    return tuple(
        pl.pallas_call(
            lambda *refs: final_kernel(n, *refs),
            out_shape=[shape((n.k, n.c), F32)] * 2,
            scratch_shapes=[
                pltpu.VMEM((n.remote, lanes), F32),
                pltpu.VMEM((up(n.bits * n.hs, 128), n.rows), F32),
                pltpu.VMEM((n.k, 2 * (1 + FACES) * n.dp, n.c), BF16),
                pltpu.VMEM((n.k, FACES * n.pp, n.c), F32),
            ],
            compiler_params=params(),
            name="finish",
        )(*local, neighbor_slot, neighbor_child, levels.reshape(1, n.c), *msgs)
    )


def solution(mesh):
    cells = ("gx", "gy")
    placed = (
        (P(None, None, cells),) * 3
        + (P(cells),) * 2
        + (P(),) * 6
        + (P(cells, None, None),) * 2
        + (P(None, cells),) * 2
        + (P(None, cells, None, None),) * 2
    )
    return jax.shard_map(
        shards,
        mesh=mesh,
        in_specs=placed,
        out_specs=(P(None, cells), P(None, cells)),
        check_vma=False,
    )
```

profile of v0, /device:TPU:4, one launch (start us, length us, event | category | flops | bytes accessed | tf_op | source)
XLA Modules:
  0.0 42.5 jit_solution(3788671373650550058)
XLA Ops:
  0.6 1.7 %copy.19.refs_0_ = f32[4,27,512]{2,1,0:T(8,128)} copy(f32[4,27,512]{2,0,1:T(4,128)} %param.17) | data formatting | bytes 442368 | tf_op args[0]
  2.3 1.7 %copy.20.refs_1_ = f32[4,27,512]{2,1,0:T(8,128)} copy(f32[4,27,512]{2,0,1:T(4,128)} %param.18) | data formatting | bytes 442368 | tf_op args[1]
  4.0 2.0 %pack.1 = (f32[40,256]{1,0:T(8,128)}, f32[40,256]{1,0:T(8,128)}, f32[40,256]{1,0:T(8,128)}, f32[16,256]{1,0:T(8,128)}, f32[16,256]{1,0:T(8,128)}) custom-call(f32[4,27,512]{2,1,0:T(8,128)} %copy.19.refs_0_, f32[4,27,512]{2,1,0:T(8,128)} %copy.20.refs_1_, s32[1,8,32]{2,1,0:T(8,128)} %refs_2_.2, s32[1,2,16]{2,1,0:T(2,128)} %refs_3_.1, s32[2,1,8,8]{3,2,1,0:T(8,128)} %refs_4_.3), custom_call_target="tpu_custom_call" | custom-call | tf_op jit(solution)/shard_map/pack/pallas_call | solution.py:288
  6.1 0.0 collective-permute-start
  6.1 1.6 %collective-permute-start.1 = (f32[40,256]{1,0:T(8,128)}, f32[40,256]{1,0:T(8,128)S(1)}, u32[]{:S(2)}, u32[]{:S(2)}) collective-permute-start(f32[40,256]{1,0:T(8,128)} %get-tuple-element.26), channel_id=1, source_target_pairs={{0,2},{1,3},{2,0},{3,1},{4,6},{5,7},{6,4},{7,5},{8,10},{9,11},{10,... | collective-permute-start | bytes 122888 | tf_op jit(solution)/shard_map/ppermute | solution.py:301
  7.7 2.6 %collective-permute-start.2 = (f32[40,256]{1,0:T(8,128)}, f32[40,256]{1,0:T(8,128)S(1)}, u32[]{:S(2)}, u32[]{:S(2)}) collective-permute-start(f32[40,256]{1,0:T(8,128)} %get-tuple-element.27), channel_id=1, source_target_pairs={{0,4},{1,5},{2,6},{3,7},{4,0},{5,1},{6,2},{7,3},{8,12},{9,13},{10,... | collective-permute-start | bytes 122888 | tf_op jit(solution)/shard_map/ppermute | solution.py:301
  10.3 3.4 %collective-permute-start.3 = (f32[16,256]{1,0:T(8,128)}, f32[16,256]{1,0:T(8,128)S(1)}, u32[]{:S(2)}, u32[]{:S(2)}) collective-permute-start(f32[16,256]{1,0:T(8,128)} %get-tuple-element.28), channel_id=1, source_target_pairs={{0,8},{8,16},{16,24},{1,9},{9,17},{17,25},{2,10},{10,18},{18,26},{... | collective-permute-start | bytes 49160 | tf_op jit(solution)/shard_map/ppermute | solution.py:304
  13.6 3.3 %collective-permute-start.4 = (f32[16,256]{1,0:T(8,128)}, f32[16,256]{1,0:T(8,128)S(1)}, u32[]{:S(2)}, u32[]{:S(2)}) collective-permute-start(f32[16,256]{1,0:T(8,128)} %get-tuple-element.29), channel_id=1, source_target_pairs={{8,0},{16,8},{24,16},{9,1},{17,9},{25,17},{10,2},{18,10},{26,18},{... | collective-permute-start | bytes 49160 | tf_op jit(solution)/shard_map/ppermute | solution.py:305
  17.0 1.9 %copy.22.refs_6_ = f32[7,125,27]{2,1,0:T(8,128)} copy(f32[7,125,27]{1,0,2:T(8,128)} %param.22) | data formatting | bytes 189000 | tf_op args[5]
  18.9 1.7 %copy.21.refs_2_ = f32[4,27,512]{2,1,0:T(8,128)} copy(f32[4,27,512]{2,0,1:T(4,128)} %param.19) | data formatting | bytes 442368 | tf_op args[2]
  20.6 1.4 %copy.23.refs_7_ = f32[125,27]{1,0:T(8,128)} copy(f32[125,27]{0,1:T(8,128)} %param.23) | data formatting | bytes 27000 | tf_op args[6]
  22.1 1.4 %copy.24.refs_8_ = f32[125,27]{1,0:T(8,128)} copy(f32[125,27]{0,1:T(8,128)} %param.24) | data formatting | bytes 27000 | tf_op args[7]
  23.5 1.4 %copy.25.refs_11_ = f32[4,25,25]{2,1,0:T(8,128)} copy(f32[4,25,25]{2,0,1:T(4,128)} %param.27) | data formatting | bytes 20000 | tf_op args[10]
  24.9 9.1 %local.1 = (bf16[6,512,512]{2,1,0:T(8,128)(2,1)}, bf16[512,512]{1,0:T(8,128)(2,1)}, f32[4,128,512]{2,1,0:T(8,128)}, bf16[256,448]{1,0:T(8,128)(2,1)}, bf16[6,160...) custom-call(f32[4,27,512]{2,1,0:T(8,128)} %copy.19.refs_0_, ...), custom_call_target="tpu_custom_call" | custom-call | flops 10000000000 | bytes 10000000 | tf_op jit(solution)/shard_map/local/pallas_call | solution.py:306
  34.1 0.0 collective-permute-done.3.refs_15_
  34.1 0.0 collective-permute-done.4.refs_16_
  34.1 0.0 collective-permute-done.refs_12_
  34.2 0.0 collective-permute-done.1.refs_13_
  34.2 0.5 %copy-done.3 = f32[16,256]{1,0:T(8,128)} copy-done((f32[16,256]{1,0:T(8,128)}, f32[16,256]{1,0:T(8,128)S(1)}, u32[]{:S(2)}) %copy-start.3) | copy-done | bytes 16408
  34.7 0.0 copy-done.4
  34.7 0.0 copy-done
  34.7 0.0 copy-done.1
  34.8 0.0 copy-done.2
  34.8 7.7 %finish.1 = (f32[4,512]{1,0:T(4,128)}, f32[4,512]{1,0:T(4,128)}) custom-call(bf16[6,512,512]{2,1,0:T(8,128)(2,1)} %get-tuple-element.16.refs_0_, bf16[512,512]{1,0:T(8,128)(2,1)} %get-tuple-element.17.refs_1_, f32[4,128,512]{2,1,0:T(8,128)} %get-tuple-element.18.refs_2_, bf16[256,448]{1,0:T(8,128)(2,1)} %get-tuple-element.19.refs_3_, ...), custom_call_target="tpu_custom_call" | custom-call | tf_op jit(solution)/shard_map/finish/pallas_call | solution.py:333
  (6 shorter events, 0.0 us)
Async XLA Ops:
  6.1 28.1 %collective-permute-start = (f32[40,256]{1,0:T(8,128)}, f32[40,256]{1,0:T(8,128)S(1)}, u32[]{:S(2)}, u32[]{:S(2)}) collective-permute-start(f32[40,256]{1,0:T(8,128)} %get-tuple-element.25), channel_id=1, source_target_pairs={{0,1},{1,0},{2,3},{3,2},{4,5},{5,4},{6,7},{7,6},{8,9},{9,8},{10,11... | collective-permute-start | bytes 122888 | tf_op jit(solution)/shard_map/ppermute | solution.py:301
  6.1 28.1 %collective-permute-start.1 = (f32[40,256]{1,0:T(8,128)}, f32[40,256]{1,0:T(8,128)S(1)}, u32[]{:S(2)}, u32[]{:S(2)}) collective-permute-start(f32[40,256]{1,0:T(8,128)} %get-tuple-element.26), channel_id=1, source_target_pairs={{0,2},{1,3},{2,0},{3,1},{4,6},{5,7},{6,4},{7,5},{8,10},{9,11},{10,... | collective-permute-start | bytes 122888 | tf_op jit(solution)/shard_map/ppermute | solution.py:301
  7.7 26.5 %collective-permute-start.2 = (f32[40,256]{1,0:T(8,128)}, f32[40,256]{1,0:T(8,128)S(1)}, u32[]{:S(2)}, u32[]{:S(2)}) collective-permute-start(f32[40,256]{1,0:T(8,128)} %get-tuple-element.27), channel_id=1, source_target_pairs={{0,4},{1,5},{2,6},{3,7},{4,0},{5,1},{6,2},{7,3},{8,12},{9,13},{10,... | collective-permute-start | bytes 122888 | tf_op jit(solution)/shard_map/ppermute | solution.py:301
  10.3 23.8 %collective-permute-start.3 = (f32[16,256]{1,0:T(8,128)}, f32[16,256]{1,0:T(8,128)S(1)}, u32[]{:S(2)}, u32[]{:S(2)}) collective-permute-start(f32[16,256]{1,0:T(8,128)} %get-tuple-element.28), channel_id=1, source_target_pairs={{0,8},{8,16},{16,24},{1,9},{9,17},{17,25},{2,10},{10,18},{18,26},{... | collective-permute-start | bytes 49160 | tf_op jit(solution)/shard_map/ppermute | solution.py:304
  13.6 20.5 %collective-permute-start.4 = (f32[16,256]{1,0:T(8,128)}, f32[16,256]{1,0:T(8,128)S(1)}, u32[]{:S(2)}, u32[]{:S(2)}) collective-permute-start(f32[16,256]{1,0:T(8,128)} %get-tuple-element.29), channel_id=1, source_target_pairs={{8,0},{16,8},{24,16},{9,1},{17,9},{25,17},{10,2},{18,10},{26,18},{... | collective-permute-start | bytes 49160 | tf_op jit(solution)/shard_map/ppermute | solution.py:305
  34.1 0.6 %copy-start.3 = (f32[16,256]{1,0:T(8,128)}, f32[16,256]{1,0:T(8,128)S(1)}, u32[]{:S(2)}) copy-start(f32[16,256]{1,0:T(8,128)S(1)} %collective-permute-done.3.refs_15_) | copy-start | bytes 49156
  34.1 0.6 %copy-start.4 = (f32[16,256]{1,0:T(8,128)}, f32[16,256]{1,0:T(8,128)S(1)}, u32[]{:S(2)}) copy-start(f32[16,256]{1,0:T(8,128)S(1)} %collective-permute-done.4.refs_16_) | copy-start | bytes 49156
  34.1 0.6 %copy-start = (f32[40,256]{1,0:T(8,128)}, f32[40,256]{1,0:T(8,128)S(1)}, u32[]{:S(2)}) copy-start(f32[40,256]{1,0:T(8,128)S(1)} %collective-permute-done.refs_12_) | copy-start | bytes 122884
  34.2 0.6 %copy-start.1 = (f32[40,256]{1,0:T(8,128)}, f32[40,256]{1,0:T(8,128)S(1)}, u32[]{:S(2)}) copy-start(f32[40,256]{1,0:T(8,128)S(1)} %collective-permute-done.1.refs_13_) | copy-start | bytes 122884
  34.2 0.6 %copy-start.2 = (f32[40,256]{1,0:T(8,128)}, f32[40,256]{1,0:T(8,128)S(1)}, u32[]{:S(2)}) copy-start(f32[40,256]{1,0:T(8,128)S(1)} %collective-permute-done.2.refs_14_) | copy-start | bytes 122884
where the time goes:
time: 43 us; the launch traced here: 42.5 us
  Pallas kernels  18.9 us (44%)
  local copies, waits for them, and re-layouts  12 us (28%)
  starting transfers between devices  10.9 us (25%)
  between operations  0.73 us (2%)
    unnamed x17, local copies, waits for them, and re-layouts  12 us
    pallas_call x1, Pallas kernels, shards(): pl.pallas_call(lambda *refs: local_kernel(n, *refs), out_shape=[shape((FA...  9.14 us
    pallas_call x1, Pallas kernels, shards(): pl.pallas_call(lambda *refs: final_kernel(n, *refs), out_shape=[shape((n....  7.74 us
    ppermute x3, starting transfers between devices, shards(): msgs.append(lax.ppermute(sent[b], 'gy', pairs))  4.2 us
    ppermute x1, starting transfers between devices, shards(): msgs.append(lax.ppermute(sent[n.bits + 1], 'gx', rising))  3.38 us
    ppermute x1, starting transfers between devices, shards(): msgs.append(lax.ppermute(sent[n.bits], 'gx', [(j, i) for i, j in rising]))  3.34 us
    pallas_call x1, Pallas kernels, shards(): pl.pallas_call(lambda *refs: pack_kernel(n, *refs), out_shape=[shape((n.m...  2.03 us
  transfers between devices with their start and end apart: 5, of which 0 were waited for; matrix products, arithmetic and copies ran while one was open for 19% of the time, Pallas kernels for 22%

commit v1 on v0

--- a/solution.py
+++ b/solution.py
@@ -81,8 +81,8 @@
     own = lax.axis_index("gy")
     data[...] = jnp.zeros(data.shape, F32)
     for k in range(n.k):
-        data[k * n.dp : k * n.dp + n.d, :] = primal[k]
-        data[n.rows + k * n.dp : n.rows + k * n.dp + n.d, :] = adjoint[k]
+        data[k * n.dp : k * n.dp + n.d, :] = primal[:, k, :]
+        data[n.rows + k * n.dp : n.rows + k * n.dp + n.d, :] = adjoint[:, k, :]
     for b in range(n.bits):
         partner = own ^ (1 << b)
         g = column(ghost[0, pl.ds(partner, 1), :])
@@ -109,20 +109,20 @@
     own = lax.axis_index("gy")
     data[...] = jnp.zeros(data.shape, F32)
     for k in range(n.k):
-        data[k * n.dp : k * n.dp + n.d, :] = primal[k]
-        data[n.rows + k * n.dp : n.rows + k * n.dp + n.d, :] = adjoint[k]
+        data[k * n.dp : k * n.dp + n.d, :] = primal[:, k, :]
+        data[n.rows + k * n.dp : n.rows + k * n.dp + n.d, :] = adjoint[:, k, :]
     hi, lo = split(data[...])
     both = jnp.concatenate([hi, lo], axis=0)
     own2[...] = both
     for f in range(FACES):
         pick = onehot(slots[f : f + 1, :] == iota((n.c, n.c), 0))
         gathered[f] = dot(both, pick).astype(BF16)
-    i_hi, i_lo = split(interp[...])
-    s_hi, s_lo = split(stiffness[...])
+    i_hi, i_lo = split(interp[...].T)
+    s_hi, s_lo = split(stiffness[...].T)
     coeff = coefficient[...]
     for k in range(n.k):
-        src_hi, src_lo = split(source[k])
-        u_hi, u_lo = split(primal[k] * coeff)
+        src_hi, src_lo = split(source[:, k, :])
+        u_hi, u_lo = split(primal[:, k, :] * coeff)
         res = dot(i_hi, src_hi) + dot(i_hi, src_lo) + dot(i_lo, src_hi)
         res = res - (dot(s_hi, u_hi) + dot(s_hi, u_lo) + dot(s_lo, u_hi))
         residual[k, : n.q, :] = res
@@ -132,7 +132,7 @@
     acc_hi = jnp.zeros((n.q, width), F32)
     acc_lo = jnp.zeros((n.q, width), F32)
     for m in range(1 + FACES):
-        w_hi, w_lo = split(recon[m])
+        w_hi, w_lo = split(recon[:, m, :].T)
         acc_hi += dot(w_hi, placed_at(n.d, width, (2 * m * n.dp, (2 * m + 1) * n.dp)))
         acc_lo += dot(w_lo, placed_at(n.d, width, (2 * m * n.dp,)))
     weights[...] = jnp.zeros(weights.shape, F32)
@@ -141,8 +141,8 @@
     rw[...] = weights[...].astype(BF16)
     stack[...] = jnp.zeros(stack.shape, F32)
     for h in range(CHILDREN):
-        stack[0, h * n.pp : h * n.pp + n.p, : n.p] = child[h]
-        stack[3, h * n.pp : h * n.pp + n.p, : n.p] = child[h].T
+        stack[0, h * n.pp : h * n.pp + n.p, : n.p] = child[:, h, :]
+        stack[3, h * n.pp : h * n.pp + n.p, : n.p] = child[:, h, :].T
     width = mw.shape[2]
     for f in range(FACES):
         child_rows = stack[0, : CHILDREN * n.pp, : n.p]
@@ -284,6 +284,10 @@
 ):
     n = Sizes(primal, ghost_send, edge_send, hang_send, recon, flux, lax.axis_size("gy"))
     shape = jax.ShapeDtypeStruct
+    primal, adjoint, source, child_interp = (
+        jnp.transpose(x, (1, 0, 2)) for x in (primal, adjoint, source, child_interp)
+    )
+    recon = jnp.transpose(recon, (2, 0, 1))
     lanes = 2 * n.rows
     sent = pl.pallas_call(
         lambda *refs: pack_kernel(n, *refs),
@@ -327,7 +331,7 @@
         name="local",
     )(
         primal, adjoint, source, coefficient.reshape(1, n.c), neighbor_slot, hang_recv,
-        recon, stiffness, interp, flux, face_eval, child_interp,
+        recon, stiffness.T, interp.T, flux, face_eval, child_interp,
     )
     return tuple(
         pl.pallas_call(

time: 43 us -> 32 us (0.74)
  local copies, waits for them, and re-layouts: 12 us -> 0.6 us
  Pallas kernels: 18.9 us -> 19.4 us
    unnamed x17 -> x10, local copies, waits for them, and re-layouts: 12 us -> 0.6 us
  transfers between devices with their start and end apart: 5 -> 5, of which waited for: 0 -> 0; matrix products, arithmetic and copies ran while one was open for 19% -> 0% of each run, Pallas kernels for 22% -> 30%
where the time goes in v1:
time: 32 us; the launch traced here: 31.7 us
  Pallas kernels  19.4 us (61%)
  starting transfers between devices  11 us (34%)
  between operations  0.73 us (2%)
  local copies, waits for them, and re-layouts  0.6 us (2%)
    pallas_call x1, Pallas kernels, shards(): pl.pallas_call(lambda *refs: local_kernel(n, *refs), out_shape=[shape((FA...  9.55 us
    pallas_call x1, Pallas kernels, shards(): pl.pallas_call(lambda *refs: final_kernel(n, *refs), out_shape=[shape((n....  7.74 us
    ppermute x3, starting transfers between devices, shards(): msgs.append(lax.ppermute(sent[b], 'gy', pairs))  4.3 us
    ppermute x1, starting transfers between devices, shards(): msgs.append(lax.ppermute(sent[n.bits + 1], 'gx', rising))  3.39 us
    ppermute x1, starting transfers between devices, shards(): msgs.append(lax.ppermute(sent[n.bits], 'gx', [(j, i) for i, j in rising]))  3.34 us
    pallas_call x1, Pallas kernels, shards(): pl.pallas_call(lambda *refs: pack_kernel(n, *refs), out_shape=[shape((n.m...  2.07 us
  transfers between devices with their start and end apart: 5, of which 0 were waited for; matrix products, arithmetic and copies ran while one was open for 0% of the time, Pallas kernels for 30%

profile of v1, /device:TPU:4, one launch (start us, length us, event | category | flops | bytes accessed | tf_op | source)
XLA Modules:
  0.0 31.7 jit_solution(13689752016014525378)
XLA Ops:
  0.6 2.1 %pack.1 = (f32[40,256]{1,0:T(8,128)}, f32[40,256]{1,0:T(8,128)}, f32[40,256]{1,0:T(8,128)}, f32[16,256]{1,0:T(8,128)}, f32[16,256]{1,0:T(8,128)}) custom-call(f32[27,4,512]{2,1,0:T(4,128)} %bitcast.9, f32[27,4,512]{2,1,0:T(4,128)} %bitcast.11, s32[1,8,32]{2,1,0:T(8,128)} %refs_2_.1, s32[1,2,16]{2,1,0:T(2,128)} %refs_3_.1, s32[2,1,8,8]{3,2,1,0:T(8,128)} %refs_4_.3), custom_call_target="tpu_custom_call" | custom-call | tf_op jit(solution)/shard_map/pack/pallas_call | solution.py:292
  2.7 3.4 %collective-permute-start.3 = (f32[16,256]{1,0:T(8,128)}, f32[16,256]{1,0:T(8,128)S(1)}, u32[]{:S(2)}, u32[]{:S(2)}) collective-permute-start(f32[16,256]{1,0:T(8,128)} %get-tuple-element.28), channel_id=1, source_target_pairs={{0,8},{8,16},{16,24},{1,9},{9,17},{17,25},{2,10},{10,18},{18,26},{... | collective-permute-start | bytes 49160 | tf_op jit(solution)/shard_map/ppermute | solution.py:308
  6.1 3.3 %collective-permute-start.4 = (f32[16,256]{1,0:T(8,128)}, f32[16,256]{1,0:T(8,128)S(1)}, u32[]{:S(2)}, u32[]{:S(2)}) collective-permute-start(f32[16,256]{1,0:T(8,128)} %get-tuple-element.29), channel_id=1, source_target_pairs={{8,0},{16,8},{24,16},{9,1},{17,9},{25,17},{10,2},{18,10},{26,18},{... | collective-permute-start | bytes 49160 | tf_op jit(solution)/shard_map/ppermute | solution.py:309
  9.4 0.1 collective-permute-start
  9.5 1.6 %collective-permute-start.1 = (f32[40,256]{1,0:T(8,128)}, f32[40,256]{1,0:T(8,128)S(1)}, u32[]{:S(2)}, u32[]{:S(2)}) collective-permute-start(f32[40,256]{1,0:T(8,128)} %get-tuple-element.26), channel_id=1, source_target_pairs={{0,2},{1,3},{2,0},{3,1},{4,6},{5,7},{6,4},{7,5},{8,10},{9,11},{10,... | collective-permute-start | bytes 122888 | tf_op jit(solution)/shard_map/ppermute | solution.py:305
  11.2 2.6 %collective-permute-start.2 = (f32[40,256]{1,0:T(8,128)}, f32[40,256]{1,0:T(8,128)S(1)}, u32[]{:S(2)}, u32[]{:S(2)}) collective-permute-start(f32[40,256]{1,0:T(8,128)} %get-tuple-element.27), channel_id=1, source_target_pairs={{0,4},{1,5},{2,6},{3,7},{4,0},{5,1},{6,2},{7,3},{8,12},{9,13},{10,... | collective-permute-start | bytes 122888 | tf_op jit(solution)/shard_map/ppermute | solution.py:305
  13.8 9.6 %local.1 = (bf16[6,512,512]{2,1,0:T(8,128)(2,1)}, bf16[512,512]{1,0:T(8,128)(2,1)}, f32[4,128,512]{2,1,0:T(8,128)}, bf16[256,448]{1,0:T(8,128)(2,1)}, bf16[6,160...) custom-call(f32[27,4,512]{2,1,0:T(4,128)} %bitcast.10, ...), custom_call_target="tpu_custom_call" | custom-call | flops 10000000000 | bytes 10000000 | tf_op jit(solution)/shard_map/local/pallas_call | solution.py:310
  23.3 0.0 collective-permute-done.3.refs_15_
  23.3 0.0 copy-start.3
  23.3 0.0 collective-permute-done.4.refs_16_
  23.3 0.0 copy-start.4
  23.3 0.0 collective-permute-done.refs_12_
  23.4 0.0 copy-start
  23.4 0.0 collective-permute-done.1.refs_13_
  23.4 0.0 copy-start.1
  23.4 0.0 collective-permute-done.2.refs_14_
  23.4 0.0 copy-start.2
  23.4 0.5 %copy-done.3 = f32[16,256]{1,0:T(8,128)} copy-done((f32[16,256]{1,0:T(8,128)}, f32[16,256]{1,0:T(8,128)S(1)}, u32[]{:S(2)}) %copy-start.3) | copy-done | bytes 16408
  23.9 0.0 copy-done.4
  23.9 0.0 copy-done
  24.0 0.0 copy-done.1
  24.0 0.0 copy-done.2
  24.0 7.7 %finish.1 = (f32[4,512]{1,0:T(4,128)}, f32[4,512]{1,0:T(4,128)}) custom-call(bf16[6,512,512]{2,1,0:T(8,128)(2,1)} %get-tuple-element.16.refs_0_, bf16[512,512]{1,0:T(8,128)(2,1)} %get-tuple-element.17.refs_1_, f32[4,128,512]{2,1,0:T(8,128)} %get-tuple-element.18.refs_2_, bf16[256,448]{1,0:T(8,128)(2,1)} %get-tuple-element.19.refs_3_, ...), custom_call_target="tpu_custom_call" | custom-call | tf_op jit(solution)/shard_map/finish/pallas_call | solution.py:337
Async XLA Ops:
  2.7 20.6 %collective-permute-start.3 = (f32[16,256]{1,0:T(8,128)}, f32[16,256]{1,0:T(8,128)S(1)}, u32[]{:S(2)}, u32[]{:S(2)}) collective-permute-start(f32[16,256]{1,0:T(8,128)} %get-tuple-element.28), channel_id=1, source_target_pairs={{0,8},{8,16},{16,24},{1,9},{9,17},{17,25},{2,10},{10,18},{18,26},{... | collective-permute-start | bytes 49160 | tf_op jit(solution)/shard_map/ppermute | solution.py:308
  6.1 17.2 %collective-permute-start.4 = (f32[16,256]{1,0:T(8,128)}, f32[16,256]{1,0:T(8,128)S(1)}, u32[]{:S(2)}, u32[]{:S(2)}) collective-permute-start(f32[16,256]{1,0:T(8,128)} %get-tuple-element.29), channel_id=1, source_target_pairs={{8,0},{16,8},{24,16},{9,1},{17,9},{25,17},{10,2},{18,10},{26,18},{... | collective-permute-start | bytes 49160 | tf_op jit(solution)/shard_map/ppermute | solution.py:309
  9.4 13.9 %collective-permute-start = (f32[40,256]{1,0:T(8,128)}, f32[40,256]{1,0:T(8,128)S(1)}, u32[]{:S(2)}, u32[]{:S(2)}) collective-permute-start(f32[40,256]{1,0:T(8,128)} %get-tuple-element.25), channel_id=1, source_target_pairs={{0,1},{1,0},{2,3},{3,2},{4,5},{5,4},{6,7},{7,6},{8,9},{9,8},{10,11... | collective-permute-start | bytes 122888 | tf_op jit(solution)/shard_map/ppermute | solution.py:305
  9.5 13.8 %collective-permute-start.1 = (f32[40,256]{1,0:T(8,128)}, f32[40,256]{1,0:T(8,128)S(1)}, u32[]{:S(2)}, u32[]{:S(2)}) collective-permute-start(f32[40,256]{1,0:T(8,128)} %get-tuple-element.26), channel_id=1, source_target_pairs={{0,2},{1,3},{2,0},{3,1},{4,6},{5,7},{6,4},{7,5},{8,10},{9,11},{10,... | collective-permute-start | bytes 122888 | tf_op jit(solution)/shard_map/ppermute | solution.py:305
  11.2 12.2 %collective-permute-start.2 = (f32[40,256]{1,0:T(8,128)}, f32[40,256]{1,0:T(8,128)S(1)}, u32[]{:S(2)}, u32[]{:S(2)}) collective-permute-start(f32[40,256]{1,0:T(8,128)} %get-tuple-element.27), channel_id=1, source_target_pairs={{0,4},{1,5},{2,6},{3,7},{4,0},{5,1},{6,2},{7,3},{8,12},{9,13},{10,... | collective-permute-start | bytes 122888 | tf_op jit(solution)/shard_map/ppermute | solution.py:305
  23.3 0.6 %copy-start.3 = (f32[16,256]{1,0:T(8,128)}, f32[16,256]{1,0:T(8,128)S(1)}, u32[]{:S(2)}) copy-start(f32[16,256]{1,0:T(8,128)S(1)} %collective-permute-done.3.refs_15_) | copy-start | bytes 49156
  23.3 0.6 %copy-start.4 = (f32[16,256]{1,0:T(8,128)}, f32[16,256]{1,0:T(8,128)S(1)}, u32[]{:S(2)}) copy-start(f32[16,256]{1,0:T(8,128)S(1)} %collective-permute-done.4.refs_16_) | copy-start | bytes 49156
  23.4 0.6 %copy-start = (f32[40,256]{1,0:T(8,128)}, f32[40,256]{1,0:T(8,128)S(1)}, u32[]{:S(2)}) copy-start(f32[40,256]{1,0:T(8,128)S(1)} %collective-permute-done.refs_12_) | copy-start | bytes 122884
  23.4 0.6 %copy-start.1 = (f32[40,256]{1,0:T(8,128)}, f32[40,256]{1,0:T(8,128)S(1)}, u32[]{:S(2)}) copy-start(f32[40,256]{1,0:T(8,128)S(1)} %collective-permute-done.1.refs_13_) | copy-start | bytes 122884
  23.4 0.6 %copy-start.2 = (f32[40,256]{1,0:T(8,128)}, f32[40,256]{1,0:T(8,128)S(1)}, u32[]{:S(2)}) copy-start(f32[40,256]{1,0:T(8,128)S(1)} %collective-permute-done.2.refs_14_) | copy-start | bytes 122884
